TPU v7x, 32 devices: a whole 2x2x4 slice. The times are simulated.
32 devices in a mesh: dp: 8 (over y, x, core), tm: 4 (over z).
Axes of the slice: x: 2, y: 2, z: 4, core: 2. Of those that a mesh axis runs over, the one named last changes fastest.
Arguments:
- tokens: bfloat16 [8, 4, 256, 1024], P('dp', 'tm'), may hold values from -6 to 6
- gain: bfloat16 [1024], replicated, may hold values from 0.25 to 1.75
- w_qkv: bfloat16 [1024, 3072], P('dp'), may hold values from -0.1875 to 0.1875
- w_out: bfloat16 [1024, 1024], P('dp'), may hold values from -0.1875 to 0.1875
- w_pair: float32 [2, 1024, 32], replicated, may hold values from -3 to 3
- codebook: float32 [8, 32], replicated, may hold values from -5 to 5
- codes: int32 [8, 4, 1], P('dp', 'tm'), may hold values from 0 to 7
Outputs:
- grad_tokens: bfloat16 [8, 4, 256, 1024], P('dp', 'tm')
- grad_pair: float32 [2, 1024, 32], replicated
- codebook_step: float32 [8, 32], replicated
Inputs may be any that keep to these rules, and one draw needn't show every extreme that they name: Every one of the 8 codes is assigned to some clip frame.
All inputs are finite; a program needn't handle non-finite values.
Results may differ from a plain program's by a relative error of at most 0.014.
Values may be sent and summed in bfloat16 or wider, within the bound.
A program may use at most 64 MiB of HBM per device.

v0:
```python
import jax
import jax.numpy as jnp
from jax import lax
from jax.sharding import PartitionSpec as P

D = 1024
HEAD_DIM = 64
CODES = 8
PATCHES = 256


EPS = 1e-06
BETA = 0.25


def passed_along(value, axis, by):
    count = lax.axis_size(axis)
    pairs = [(i, i + by) for i in range(count) if 0 <= i + by < count]
    return lax.ppermute(value, axis, pairs)


def normalize(xf, gain):
    scale = lax.rsqrt(jnp.mean(xf * xf, axis=-1, keepdims=True) + EPS)
    return (xf * scale * gain.astype(jnp.float32)).astype(jnp.bfloat16)


def project(normed, weight):
    shape = normed.shape
    flat = jnp.dot(normed.reshape(-1, shape[-1]), weight, preferred_element_type=jnp.float32)
    return flat.astype(jnp.bfloat16).reshape(shape[:-1] + (3, shape[-1]))


def attend(qkv):
    clips, frames, patches, _, width = qkv.shape
    local_heads = width // HEAD_DIM
    parts = qkv.reshape(clips, frames, patches, 3, local_heads, HEAD_DIM)
    query = parts[:, :, :, 0].astype(jnp.float32)
    keys = parts[:, :, :, 1].astype(jnp.float32)
    values = parts[:, :, :, 2].astype(jnp.float32)
    scores = jnp.einsum("cfphd,cgphd->cphfg", query, keys) * HEAD_DIM ** (-0.5)
    causal = jnp.arange(frames)[:, None] >= jnp.arange(frames)[None, :]
    scores = jnp.where(causal, scores, -1e30)
    weights = jax.nn.softmax(scores, axis=-1).astype(jnp.bfloat16)
    mixed = jnp.einsum("cphfg,cgphd->cfphd", weights.astype(jnp.float32), values)
    return mixed.reshape(clips, frames, patches, width).astype(jnp.bfloat16)


def output(xf, attended, weight):
    shape = xf.shape
    moved = jnp.dot(attended.reshape(-1, shape[-1]), weight, preferred_element_type=jnp.float32)
    return jnp.mean(xf + moved.reshape(shape), axis=2)


def local(tokens, gain, w_qkv, w_out, w_pair, codebook, codes):
    xf = tokens.astype(jnp.float32)
    groups = lax.axis_size("tm")
    full_out = w_out
    full_qkv, full_out = (
        lax.all_gather(w_qkv, "dp", axis=0, tiled=True),
        lax.all_gather(w_out, "dp", axis=0, tiled=True),
    )
    normed, norm_back = jax.vjp(lambda value: normalize(value, gain), xf)
    regrouped = lax.all_to_all(normed, "tm", split_axis=2, concat_axis=1, tiled=True)
    qkv, qkv_back = jax.vjp(lambda value: project(value, full_qkv), regrouped)
    attended, attend_back = jax.vjp(attend, qkv)
    lifted = attended[:, :, None]
    returned = lax.all_to_all(lifted, "tm", split_axis=1, concat_axis=2, tiled=True)
    clips_here, frames_here = (returned.shape[0], returned.shape[1])
    local_out = returned.reshape(clips_here, frames_here, -1, D)
    pooled, out_back = jax.vjp(lambda first, second: output(first, second, full_out), xf, local_out)
    following = passed_along(pooled, "tm", -1)
    flat_now = pooled.reshape(-1, D)
    flat_next = following.reshape(-1, D)
    highest = lax.Precision.HIGHEST
    action = jnp.dot(flat_now, w_pair[0], precision=highest) + jnp.dot(
        flat_next, w_pair[1], precision=highest
    )
    onehot = (codes.reshape(-1)[:, None] == jnp.arange(CODES)[None, :]).astype(jnp.float32)
    quantized = jnp.dot(onehot, codebook, precision=highest)
    diff = action - quantized
    d_action = 2.0 * BETA * diff
    d_quant = -2.0 * diff
    pair_part = jnp.stack(
        [
            jnp.dot(flat_now.T, d_action, precision=highest),
            jnp.dot(flat_next.T, d_action, precision=highest),
        ]
    )
    code_part = jnp.dot(onehot.T, d_quant, precision=highest)
    count_part = jnp.sum(onehot, axis=0)
    grad_pair, code_total, count = lax.psum((pair_part, code_part, count_part), ("dp", "tm"))
    codebook_step = code_total / count[:, None]
    d_own = jnp.dot(d_action, w_pair[0].T, precision=highest).reshape(pooled.shape)
    d_next = jnp.dot(d_action, w_pair[1].T, precision=highest).reshape(pooled.shape)
    carried = passed_along(d_next, "tm", 1)
    d_pooled = (d_own + carried) * PATCHES
    d_resid, d_local = out_back(d_pooled)
    clips_here, frames_here, rows_here = (d_local.shape[0], d_local.shape[1], d_local.shape[2])
    spread = d_local.reshape(clips_here, frames_here, groups, rows_here // groups, D)
    gathered_back = lax.all_to_all(spread, "tm", split_axis=2, concat_axis=1, tiled=True)
    d_attended = gathered_back.reshape(attended.shape)
    (d_qkv,) = attend_back(d_attended)
    (d_regrouped,) = qkv_back(d_qkv)
    d_normed = lax.all_to_all(d_regrouped, "tm", split_axis=1, concat_axis=2, tiled=True)
    (d_through,) = norm_back(d_normed)
    grad_tokens = (d_resid + d_through).astype(jnp.bfloat16)
    return (grad_tokens, grad_pair, codebook_step)


def solution(mesh):
    placed = (
        P("dp", "tm", None, None),
        P(),
        P("dp", None),
        P("dp", None),
        P(),
        P(),
        P("dp", "tm", None),
    )
    return jax.shard_map(
        local,
        mesh=mesh,
        in_specs=placed,
        out_specs=(P("dp", "tm", None, None), P(), P()),
        check_vma=False,
    )
```

profile of v0, /device:TPU:0, one launch (start us, length us, event | category | flops | bytes accessed | tf_op | source)
XLA Modules:
  0.0 300.7 jit_solution(16761562726995000602)
XLA Ops:
  7.2 0.0 copy-start
  7.2 0.0 all-gather.3.cloned.1.call-start
  7.2 0.7 all-gather.3.cloned.1.call-update
  7.9 0.7 convert_element_type.110
  8.6 1.2 fusion.15
  9.8 1.2 fusion.17
  11.1 0.8 copy.83
  11.9 0.5 broadcast.182
  12.4 3.9 %reduce.9 = bf16[256,1024]{1,0:T(8,128)(2,1)S(1)} reduce(bf16[256,1,1,1024]{3,2,1,0:T(2,128)(2,1)S(1)} %bitcast.152, bf16[]{:T(256)} %broadcast.182), dimensions={1,2}, to_apply=%bitcast.147.reduce_sub_computation | reduce | bytes 1048578
  16.4 1.2 reshape.366
  17.5 6.3 %all-to-all-start = ((bf16[4,2,32768]{2,1,0:T(2,128)(2,1)}), bf16[4,2,32768]{2,1,0:T(2,128)(2,1)S(1)}, u32[]{:S(2)}, u32[]{:S(2)}) async-start(bf16[4,2,32768]{2,1,0:T(2,128)(2,1)} %reshape.366), calls=%async_computation | async-start | bytes 1048576 | tf_op jit(solution)/shard_map/all_to_all | solution.py:63
  23.9 0.7 all-gather.5.cloned.1.call-update
  24.6 13.7 %all-to-all-done = bf16[4,2,32768]{2,1,0:T(2,128)(2,1)S(1)} async-done(((bf16[4,2,32768]{2,1,0:T(2,128)(2,1)}), bf16[4,2,32768]{2,1,0:T(2,128)(2,1)S(1)}, u32[]{:S(2)}, u32[]{:S(2)}) %all-to-all-start) | async-done | bytes 524320 | tf_op jit(solution)/shard_map/all_to_all | solution.py:63
  38.4 0.5 reshape.367
  38.9 19.1 %all-gather.3.cloned.1.call-done = bf16[1024,3072]{1,0:T(8,128)(2,1)} async-done(((bf16[128,3072]{1,0:T(8,128)(2,1)}), bf16[1024,3072]{1,0:T(8,128)(2,1)}) %all-gather.3.cloned.1.call-update) | async-done | bytes 6291472 | tf_op jit(solution)/shard_map/all_gather | solution.py:59
  58.0 5.8 %convolution_convert_fusion = bf16[256,3072]{1,0:T(8,128)(2,1)} fusion(bf16[1024,3072]{1,0:T(8,128)(2,1)} %all-gather.3.cloned.1.call-done, bf16[1,1,256,1024]{3,1,0,2:T(2,128)(2,1)S(1)} %bitcast.154), kind=kOutput, calls=%fused_computation.1 | convolution fusion | flops 1611399168 | bytes 8388608 | tf_op jit(solution)/shard_map/jvp()/dot_general | solution.py:29
  63.8 3.7 %reshape.339 = bf16[1,4,64,3,16,64]{5,4,3,2,1,0:T(8,128)(2,1)S(1)} reshape(bf16[256,3072]{1,0:T(8,128)(2,1)} %convolution_convert_fusion) | data formatting | bytes 3145728 | tf_op jit(solution)/shard_map/jvp()/reshape;jvp()/reshape | solution.py:36
  67.5 1.9 fusion.43
  69.4 5.3 %fusion.44 = (f32[64,16,4]{2,1,0:T(8,128)S(1)}, f32[64,16,4,4]{2,3,1,0:T(4,128)S(1)}) fusion(pred[4,4]{0,1:T(4,128)(4,1)S(1)} %iota_compare_fusion, bf16[1,4,64,1,16,64]{5,4,3,2,1,0:T(8,128)(2,1)} %get-tuple-element.6, bf16[1,4,64,1,16,64]{5,4,3,2,1,0:T(8,128)(2,1)} %get-tuple-element.7), kind=kOutput, calls=%fused_computation.88 | convolution fusion | flops 2162691 | bytes 1130512 | tf_op jit(solution)/shard_map/jvp()/sub | solution.py:43
  74.7 0.6 divide_convert_fusion
  75.4 1.0 copy-done.3
  76.4 1.6 fusion.5
  78.0 0.0 copy-start.1
  78.0 1.2 copy.40
  79.2 2.6 convert_element_type.117
  81.8 4.6 %all-to-all-start.1 = ((bf16[1,4,1,64,1024]{4,3,2,0,1:T(8,128)(2,1)}), bf16[1,4,1,64,1024]{4,3,2,0,1:T(8,128)(2,1)}, u32[]{:S(2)}, u32[]{:S(2)}) async-start(bf16[1,4,1,64,1024]{4,3,2,0,1:T(8,128)(2,1)} %bitcast.153), calls=%async_computation.1 | async-start | bytes 1048576 | tf_op jit(solution)/shard_map/all_to_all | solution.py:67
  87.1 0.1 convolution_bitcast_fusion.3
  87.2 0.5 all-gather.5.cloned.1.call-done
  87.7 13.7 %all-to-all-done.1 = bf16[1,4,1,64,1024]{4,3,2,0,1:T(8,128)(2,1)} async-done(((bf16[1,4,1,64,1024]{4,3,2,0,1:T(8,128)(2,1)}), bf16[1,4,1,64,1024]{4,3,2,0,1:T(8,128)(2,1)}, u32[]{:S(2)}, u32[]{:S(2)}) %all-to-all-start.1) | async-done | bytes 524320 | tf_op jit(solution)/shard_map/all_to_all | solution.py:67
  101.4 2.6 fusion.9
  104.1 1.3 collective-permute-start
  105.4 0.2 convolution_bitcast_fusion.5
  105.6 4.0 %collective-permute-done = f32[1,1,1024]{2,1,0:T(1,128)S(1)} collective-permute-done((f32[1,1,1024]{2,1,0:T(1,128)S(1)}, f32[1,1,1024]{2,1,0:T(1,128)S(1)}, u32[]{:S(2)}, u32[]{:S(2)}) %collective-permute-start) | collective-permute-done | bytes 4128 | tf_op jit(solution)/shard_map/ppermute | solution.py:19
  109.6 0.2 broadcast_multiply_fusion.2
  109.8 0.2 convolution_bitcast_fusion.1
  110.0 1.7 collective-permute-start.1
  111.6 1.3 collective-permute-done.1
  113.0 0.2 fusion.10
  113.2 1.6 convolution_convert_fusion.7
  114.7 3.7 %all-to-all-start.2 = ((bf16[1,1,4,64,1024]{4,3,1,0,2:T(8,128)(2,1)}), bf16[1,1,4,64,1024]{4,3,1,0,2:T(8,128)(2,1)S(1)}, u32[]{:S(2)}, u32[]{:S(2)}) async-start(bf16[1,1,4,64,1024]{4,3,1,0,2:T(8,128)(2,1)} %bitcast.155), calls=%async_computation.2 | async-start | bytes 1048576 | tf_op jit(solution)/shard_map/all_to_all | solution.py:100
  118.4 0.9 multiply_divide_fusion
  119.3 11.2 %all-to-all-done.2 = bf16[1,1,4,64,1024]{4,3,1,0,2:T(8,128)(2,1)S(1)} async-done(((bf16[1,1,4,64,1024]{4,3,1,0,2:T(8,128)(2,1)}), bf16[1,1,4,64,1024]{4,3,1,0,2:T(8,128)(2,1)S(1)}, u32[]{:S(2)}, u32[]{:S(2)}) %all-to-all-start.2) | async-done | bytes 524320 | tf_op jit(solution)/shard_map/all_to_all | solution.py:100
  130.5 1.7 reshape.349
  132.2 2.9 fusion.6
  135.1 2.7 fusion.4
  137.9 1.4 select_multiply_fusion
  139.3 1.2 fusion.7
  140.6 1.6 fusion.8
  142.2 3.1 %pad_add_fusion = bf16[1,4,64,3,16,64]{5,1,4,2,3,0:T(4,128)(2,1)S(1)} fusion(bf16[1,4,64,1,16,64]{5,1,4,2,3,0:T(4,128)(2,1)S(1)} %fusion.8, bf16[1,4,64,1,16,64]{5,1,4,2,3,0:T(4,128)(2,1)S(1)} %fusion.7, bf16[1,4,64,1,16,64]{5,1,4,2,3,0:T(4,128)(2,1)S(1)} %fusion.6), kind=kLoop, calls=%fused_computation.2 | loop fusion | flops 1572864 | bytes 3145728 | tf_op jit(solution)/shard_map/transpose(jvp())/add_any | solution.py:37
  145.4 0.4 copy.45
  145.8 3.2 %reshape.351 = bf16[256,3072]{1,0:T(8,128)(2,1)} reshape(bf16[1,4,64,3,16,64]{5,4,3,2,1,0:T(8,128)(2,1)S(1)} %copy.45) | data formatting | bytes 3145728 | tf_op jit(solution)/shard_map/transpose(jvp())/reshape;transpose(jvp())/reshape | solution.py:30
  149.0 5.9 %convolution_convert_fusion.6 = bf16[256,1024]{1,0:T(8,128)(2,1)} fusion(bf16[256,3072]{1,0:T(8,128)(2,1)} %reshape.351, bf16[1024,3072]{1,0:T(8,128)(2,1)} %all-gather.3.cloned.1.call-done), kind=kOutput, calls=%fused_computation.29 | convolution fusion | flops 1610874880 | bytes 8388608 | tf_op jit(solution)/shard_map/transpose(jvp())/dot_general | solution.py:29
  154.9 3.6 %all-to-all-start.3 = ((bf16[1,4,64,1024]{3,2,0,1:T(8,128)(2,1)}), bf16[1,4,64,1024]{3,2,0,1:T(8,128)(2,1)S(1)}, u32[]{:S(2)}, u32[]{:S(2)}) async-start(bf16[1,4,64,1024]{3,2,0,1:T(8,128)(2,1)} %bitcast.41), calls=%async_computation.3 | async-start | bytes 1048576 | tf_op jit(solution)/shard_map/all_to_all | solution.py:104
  158.5 0.0 all-reduce.6.cloned.1.call-start
  158.5 0.1 multiply_bitcast_fusion.1
  158.6 0.7 pad_maximum_fusion
  159.4 0.0 all-reduce.6.cloned.1.call-update
  159.4 0.1 broadcast_multiply_fusion
  159.5 39.8 %all-reduce.3 = (f32[8,32]{1,0:T(8,128)S(1)}, f32[8]{0:T(128)S(1)}) all-reduce(f32[8,32]{1,0:T(8,128)S(1)} %broadcast_multiply_fusion, f32[8]{0:T(128)S(1)} %compare_convert_fusion), channel_id=1, replica_groups=mesh['dp'=8,'tm'=4] {'dp','tm'}, use_global_device_ids=true, to_apply=%region_7.8 | all-reduce | flops 264 | bytes 2112 | tf_op jit(solution)/shard_map/psum | solution.py:91
  199.3 0.7 broadcast_divide_fusion
  200.0 0.2 fusion.18
  200.2 1.1 fusion.14
  201.4 91.1 %all-reduce.6.cloned.1.call-done = f32[2,1024,32]{1,2,0:T(8,128)} async-done(((f32[2,1024,32]{1,2,0:T(8,128)}), f32[2,1024,32]{1,2,0:T(8,128)}) %all-reduce.6.cloned.1.call-update) | async-done | bytes 262160 | tf_op jit(solution)/shard_map/psum | solution.py:91
  292.5 1.7 copy.86
  (29 shorter events, 0.1 us)
Async XLA Ops:
  7.2 80.0 %copy-start = (f32[8,32]{1,0:T(8,128)S(1)}, f32[8,32]{1,0:T(8,128)}, u32[]{:S(2)}) copy-start(f32[8,32]{1,0:T(8,128)} %param.12) | copy-start | bytes 3076
  7.2 50.8 %all-gather.3.cloned.1.call-start = ((), (), s32[]{:S(2)}) async-start(), calls=%async_computation.4 | async-start | bytes 7077888 | tf_op jit(solution)/shard_map/all_gather | solution.py:59
  17.5 20.8 %all-to-all-start = ((bf16[4,2,32768]{2,1,0:T(2,128)(2,1)}), bf16[4,2,32768]{2,1,0:T(2,128)(2,1)S(1)}, u32[]{:S(2)}, u32[]{:S(2)}) async-start(bf16[4,2,32768]{2,1,0:T(2,128)(2,1)} %reshape.366), calls=%async_computation | async-start | bytes 1048576 | tf_op jit(solution)/shard_map/all_to_all | solution.py:63
  23.9 63.8 %all-gather.5.cloned.1.call-start = ((), (), s32[]{:S(2)}) async-start(), calls=%async_computation.5 | async-start | bytes 2359296 | tf_op jit(solution)/shard_map/all_gather | solution.py:60
  74.7 1.6 copy-start.8
  75.4 1.0 copy-start.3
  78.0 23.4 %copy-start.1 = (bf16[1,1,256,1024]{3,2,1,0:T(8,128)(2,1)S(1)}, bf16[1,1,256,1024]{3,2,1,0:T(8,128)(2,1)}, u32[]{:S(2)}) copy-start(bf16[1,1,256,1024]{3,2,1,0:T(8,128)(2,1)} %param.7) | copy-start | bytes 1572868
  81.8 19.6 %all-to-all-start.1 = ((bf16[1,4,1,64,1024]{4,3,2,0,1:T(8,128)(2,1)}), bf16[1,4,1,64,1024]{4,3,2,0,1:T(8,128)(2,1)}, u32[]{:S(2)}, u32[]{:S(2)}) async-start(bf16[1,4,1,64,1024]{4,3,2,0,1:T(8,128)(2,1)} %bitcast.153), calls=%async_computation.1 | async-start | bytes 1048576 | tf_op jit(solution)/shard_map/all_to_all | solution.py:67
  86.4 19.0 %copy-start.5 = (f32[2,1024,32]{1,2,0:T(8,128)S(1)}, f32[2,1024,32]{1,2,0:T(8,128)}, u32[]{:S(2)}) copy-start(f32[2,1024,32]{1,2,0:T(8,128)} %param.11) | copy-start | bytes 786436
  101.4 11.7 %copy-start.11 = (bf16[1024,1024]{1,0:T(8,128)(2,1)S(1)}, bf16[1024,1024]{1,0:T(8,128)(2,1)}, u32[]{:S(2)}) copy-start(bf16[1024,1024]{1,0:T(8,128)(2,1)} %all-gather.5.cloned.1.call-done) | copy-start | bytes 6291460
  104.1 5.5 %collective-permute-start = (f32[1,1,1024]{2,1,0:T(1,128)S(1)}, f32[1,1,1024]{2,1,0:T(1,128)S(1)}, u32[]{:S(2)}, u32[]{:S(2)}) collective-permute-start(f32[1,1,1024]{2,1,0:T(1,128)S(1)} %bitcast.156), channel_id=1, source_target_pairs={{1,0},{2,1},{3,2},{5,4},{6,5},{7,6},{9,8},{10,9},{11,10},{13,12},{... | collective-permute-start | bytes 12296 | tf_op jit(solution)/shard_map/ppermute | solution.py:19
  110.0 3.0 collective-permute-start.1
  114.7 15.8 %all-to-all-start.2 = ((bf16[1,1,4,64,1024]{4,3,1,0,2:T(8,128)(2,1)}), bf16[1,1,4,64,1024]{4,3,1,0,2:T(8,128)(2,1)S(1)}, u32[]{:S(2)}, u32[]{:S(2)}) async-start(bf16[1,1,4,64,1024]{4,3,1,0,2:T(8,128)(2,1)} %bitcast.155), calls=%async_computation.2 | async-start | bytes 1048576 | tf_op jit(solution)/shard_map/all_to_all | solution.py:100
  132.2 2.9 copy-start.4
  132.2 2.9 copy-start.9
  132.2 2.9 copy-start.10
  137.9 1.4 copy-start.7
  139.3 1.2 copy-start.6
  154.9 45.1 %copy-start.2 = (bf16[1,1,256,1024]{3,2,1,0:T(8,128)(2,1)S(1)}, bf16[1,1,256,1024]{3,2,1,0:T(8,128)(2,1)}, u32[]{:S(2)}) copy-start(bf16[1,1,256,1024]{3,2,1,0:T(8,128)(2,1)} %param.7) | copy-start | bytes 1572868
  154.9 45.1 %all-to-all-start.3 = ((bf16[1,4,64,1024]{3,2,0,1:T(8,128)(2,1)}), bf16[1,4,64,1024]{3,2,0,1:T(8,128)(2,1)S(1)}, u32[]{:S(2)}, u32[]{:S(2)}) async-start(bf16[1,4,64,1024]{3,2,0,1:T(8,128)(2,1)} %bitcast.41), calls=%async_computation.3 | async-start | bytes 1048576 | tf_op jit(solution)/shard_map/all_to_all | solution.py:104
  158.5 134.0 %all-reduce.6.cloned.1.call-start = ((), (), s32[]{:S(2)}) async-start(), calls=%async_computation.6 | async-start | bytes 524288 | tf_op jit(solution)/shard_map/psum | solution.py:91
Sparse Core Ops, SparseCore 0:
  9.9 48.1 all-gather.2
  59.9 27.7 all-gather.4
  165.4 127.0 all-reduce.5
where the time goes:
time: 301 us
  waiting for transfers between devices  156 us (52%)
  blocking collectives  39.8 us (13%)
  matrix products  32.2 us (11%)
  starting transfers between devices  21.3 us (7%)
  local copies, waits for them, and re-layouts  20.4 us (7%)
  other arithmetic  16.1 us (5%)
  between operations  14.8 us (5%)
    psum x1, waiting for transfers between devices, local(): lax.psum((pair_part, code_part, count_part), ('dp', 'tm'))  91.1 us
    psum x1, blocking collectives, local(): lax.psum((pair_part, code_part, count_part), ('dp', 'tm'))  39.8 us
    all_gather x1, waiting for transfers between devices, local(): lax.all_gather(w_qkv, 'dp', axis=0, tiled=True)  19.1 us
    all_to_all x1, waiting for transfers between devices, local(): lax.all_to_all(normed, 'tm', split_axis=2, concat_axis=1, tiled=True)  13.7 us
    all_to_all x1, waiting for transfers between devices, local(): lax.all_to_all(lifted, 'tm', split_axis=1, concat_axis=2, tiled=True)  13.7 us
    dot_general x2, matrix products, project(): jnp.dot(normed.reshape(-1, shape[-1]), weight, preferred_element_type=jnp...  11.7 us
    all_to_all x1, waiting for transfers between devices, local(): lax.all_to_all(spread, 'tm', split_axis=2, concat_axis=1, tiled=True)  11.2 us
    dot_general x3, matrix products, attend(): jnp.einsum('cphfg,cgphd->cfphd', weights.astype(jnp.float32), values)  7.25 us
  transfers between devices with their start and end apart: 9, of which 8 were waited for; matrix products, arithmetic and copies ran while one was open for 12% of the time, Pallas kernels for 0%

commit v1 on v0

v1 whole, which is shorter than its diff:
```python
import functools

import jax
import jax.numpy as jnp
from jax import lax
from jax.experimental import pallas as pl
from jax.experimental.pallas import tpu as pltpu
from jax.sharding import PartitionSpec as P

HEAD_DIM = 64
EPS = 1e-06
BETA = 0.25
LANES = 128
F32 = jnp.float32
BF16 = jnp.bfloat16
HIGH = lax.Precision.HIGHEST


def dot(a, b, ca=1, cb=0, precision=None):
    return lax.dot_general(
        a, b, (((ca,), (cb,)), ((), ())), precision=precision, preferred_element_type=F32
    )


def dot_split(a, b, cb=0):
    high = a.astype(BF16)
    rest = a - high.astype(F32)
    mid = rest.astype(BF16)
    low = (rest - mid.astype(F32)).astype(BF16)
    n = a.shape[0]
    terms = jnp.concatenate([high.astype(F32), mid.astype(F32), low.astype(F32)], axis=0)
    out = dot(terms.astype(BF16), b, 1, cb)
    return out[:n] + out[n : 2 * n] + out[2 * n :]


def bits_of(n):
    return max(n.bit_length() - 1, 0)


def ring_place(chip, n):
    b = [(chip // 2**k) % 2 for k in range(bits_of(n))]
    return sum(((sum(b[k:]) % 2) * 2**k for k in range(len(b))), 0)


def ring_chip(place, n):
    count = bits_of(n)
    b = [(place // 2**k) % 2 for k in range(count)] + [0]
    return sum((((b[k] + b[k + 1]) % 2) * 2**k for k in range(count)), 0)


def kernel(
    cfg, tokens, gain, wq_own, wo_own, w_pair, codebook, codes,
    out, pair_out, step_out,
    wq, wo, x, normed, acc, qkv, bias, probs, attended, sums, sums_all, pack, pack_all,
    d_rows, d_att, dqkv, dn_send, dn_recv, send, recv, local_sem,
):
    dp, tm, rows, patches, width, latent, n_codes = cfg
    mine = patches // tm
    total = tm * mine
    fp = sums.shape[1]
    chips = dp // 2
    half_ring = chips // 2
    i = lax.axis_index("dp")
    t = lax.axis_index("tm")
    core = i % 2
    place = ring_place(i // 2, chips)

    def device_at(p, c):
        return ring_chip((p + 2 * chips) % chips, chips) * 2 + c

    barrier = pltpu.get_barrier_semaphore()
    for r in range(1, tm):
        pl.semaphore_signal(barrier, inc=1, device_id={"dp": i, "tm": (t + r) % tm})
    for r in range(1, dp):
        pl.semaphore_signal(barrier, inc=1, device_id={"dp": (i + r) % dp, "tm": t})
    pl.semaphore_wait(barrier, tm + dp - 2)

    tags = {}

    def tag(*key):
        return tags.setdefault(key, len(tags))

    started = []

    def remote(src, dst, key, dpi, tmi):
        k = tag(*key)
        return pltpu.make_async_remote_copy(
            src_ref=src, dst_ref=dst, send_sem=send.at[k], recv_sem=recv.at[k],
            device_id={"dp": dpi, "tm": tmi},
        )

    def go(copy):
        copy.start()
        started.append(copy)

    mats = (wq, wo)
    owns = (wq_own, wo_own)
    half = rows // 2
    dirs = (1, -1)

    def piece(m, origin, h):
        return mats[m].at[pl.ds(pl.multiple_of(origin * rows + h * half, half), half)]

    def own_piece(m, h):
        return owns[m].at[pl.ds(h * half, half)]

    def main_half(d):
        return 0 if dirs[d] == 1 else 1

    def halves(d, s):
        first = main_half(d)
        return (first, 1 - first) if s < half_ring - 1 else (first,)

    def ring_copy(m, d, s, h):
        origin = device_at(place - dirs[d] * s, core)
        src = own_piece(m, h) if s == 0 else piece(m, origin, h)
        return remote(src, piece(m, origin, h), ("ring", m, d, s, h), device_at(place + dirs[d], core), t)

    def sib_copy(m, d, s, h):
        origin = device_at(place - dirs[d] * s, core)
        src = own_piece(m, h) if s == 0 else piece(m, origin, h)
        return remote(src, piece(m, origin, h), ("sib", m, d, s, h), device_at(place, 1 - core), t)

    def start_own(m):
        for n in range(2):
            for d in range(2):
                if n < len(halves(d, 0)):
                    go(ring_copy(m, d, 0, halves(d, 0)[n]))
        for h in range(2):
            go(sib_copy(m, 0, 0, h))

    def take(m, d, s, h):
        ring_copy(m, d, s, h).wait_recv()
        if s + 1 < half_ring and h in halves(d, s + 1):
            go(ring_copy(m, d, s + 1, h))
        go(sib_copy(m, d, s + 1, h))

    for r in sorted(range(1, tm), key=lambda r: -min(r, tm - r)):
        other = (t + r) % tm
        go(remote(
            tokens.at[pl.ds(pl.multiple_of(other * mine, mine), mine)],
            x.at[pl.ds(pl.multiple_of(t * mine, mine), mine)], ("tok", r), i, other,
        ))
    start_own(0)
    here = [
        pltpu.make_async_copy(wq_own, wq.at[pl.ds(pl.multiple_of(i * rows, rows), rows)], local_sem.at[0]),
        pltpu.make_async_copy(wo_own, wo.at[pl.ds(pl.multiple_of(i * rows, rows), rows)], local_sem.at[1]),
        pltpu.make_async_copy(
            tokens.at[pl.ds(pl.multiple_of(t * mine, mine), mine)],
            x.at[pl.ds(pl.multiple_of(t * mine, mine), mine)], local_sem.at[2],
        ),
    ]
    for copy in here:
        copy.start()

    row = lax.broadcasted_iota(jnp.int32, (total, total), 0)
    col = lax.broadcasted_iota(jnp.int32, (total, total), 1)
    seen = (row % mine == col % mine) & (row // mine >= col // mine)
    bias[...] = jnp.where(seen, 0.0, -1e30).astype(F32)

    def first_main(m):
        for s in range(half_ring):
            for d in range(2):
                take(m, d, s, main_half(d))

    def rest_of(m):
        for s in range(half_ring):
            for d in range(2):
                for h in halves(d, s)[1:]:
                    take(m, d, s, h)

    if half_ring > 1:
        for d in range(2):
            take(0, d, 0, main_half(d))
    start_own(1)

    for copy in here:
        copy.wait()
    for r in range(1, tm):
        remote(
            tokens.at[pl.ds(0, mine)], x.at[pl.ds(pl.multiple_of(t * mine, mine), mine)], ("tok", r), i, t
        ).wait_recv()

    block = 32

    def norm_step(b, carry):
        at = pl.ds(pl.multiple_of(b * block, block), block)
        xf = x[at, :].astype(F32)
        scale = lax.rsqrt(jnp.mean(xf * xf, axis=-1, keepdims=True) + EPS)
        normed[at, :] = (xf * scale * gain[...].astype(F32)).astype(BF16)
        return carry

    lax.fori_loop(0, total // block, norm_step, 0)

    pair = 2 * rows
    columns = 512

    def project(p, first, last):
        base = pl.multiple_of(ring_chip((p + 2 * chips) % chips, chips) * pair, pair)

        def body(n, carry):
            at = pl.ds(pl.multiple_of(n * columns, columns), columns)
            part = dot(normed[:, pl.ds(base, pair)], wq[pl.ds(base, pair), at])
            if not first:
                part = part + acc[:, at]
            if last:
                qkv[:, at] = part.astype(BF16)
            else:
                acc[:, at] = part
            return carry

        lax.fori_loop(0, 3 * width // columns, body, 0)

    def wait_sib(m, d, s, h):
        sib_copy(m, d, s, h).wait_recv()

    by_chip = pair % LANES == 0
    for h in range(2):
        wait_sib(0, 0, 0, h)
    if by_chip:
        project(place, True, chips == 1)
    for s in range(half_ring):
        for d in range(2):
            for n, h in enumerate(halves(d, s)):
                if not (half_ring > 1 and s == 0 and n == 0):
                    take(0, d, s, h)
        for d in range(2):
            for h in halves(d, s):
                wait_sib(0, d, s + 1, h)
            if by_chip and s < half_ring - 1:
                project(place - dirs[d] * (s + 1), False, False)
    if by_chip:
        project(place + half_ring, False, True)
    else:
        def whole_body(n, carry):
            at = pl.ds(pl.multiple_of(n * columns, columns), columns)
            qkv[:, at] = dot(normed[...], wq[:, at]).astype(BF16)
            return carry

        lax.fori_loop(0, 3 * width // columns, whole_body, 0)

    per = LANES // HEAD_DIM
    lane = lax.broadcasted_iota(jnp.int32, (total, LANES), 1)
    scale_q = HEAD_DIM ** (-0.5)

    def only(value, j):
        return jnp.where(lane // HEAD_DIM == j, value, jnp.zeros_like(value))

    def lanes_at(b, part):
        return pl.ds(pl.multiple_of(part * width + b * LANES, LANES), LANES)

    def forward(b, carry):
        q, k, v = (qkv[:, lanes_at(b, n)] for n in range(3))
        mixed = None
        for j in range(per):
            scores = dot(only(q, j), k, 1, 1) * scale_q + bias[...]
            e = jnp.exp(scores - jnp.max(scores, axis=-1, keepdims=True))
            w = e / jnp.sum(e, axis=-1, keepdims=True)
            probs[b * per + j] = w
            term = dot(w.astype(BF16), only(v, j))
            mixed = term if mixed is None else mixed + term
        attended[:, lanes_at(b, 0)] = mixed.astype(BF16)
        return carry

    lax.fori_loop(0, width // LANES, forward, 0)

    frow = lax.broadcasted_iota(jnp.int32, (fp, total), 0)
    fcol = lax.broadcasted_iota(jnp.int32, (fp, total), 1)
    member = jnp.where(fcol // mine == frow, 1.0, 0.0).astype(BF16)
    sums[0] = dot(member, attended[...])
    sums[1] = dot(member, x[...])
    r8 = lax.broadcasted_iota(jnp.int32, (fp, width), 0)
    l8 = lax.broadcasted_iota(jnp.int32, (fp, width), 1)
    sums[2] = jnp.where((r8 == t) & (l8 == codes[0, 0]), 1.0, 0.0).astype(F32)
    for r in range(1, tm):
        go(remote(sums, sums_all.at[t], ("sum", r), i, (t + r) % tm))

    for s in range(half_ring):
        for d in range(2):
            for h in halves(d, s):
                take(1, d, s, h)
    sums_all[t] = sums[...]
    for h in range(2):
        wait_sib(1, 0, 0, h)
    for s in range(half_ring):
        for d in range(2):
            for h in halves(d, s):
                wait_sib(1, d, s + 1, h)
    for r in range(1, tm):
        remote(sums, sums_all.at[t], ("sum", r), i, t).wait_recv()

    tot = sums_all[0]
    for r in range(1, tm):
        tot = tot + sums_all[r]
    onehot = tot[2][:, :LANES]
    pooled = tot[1] * (1.0 / patches) + dot_split(tot[0] * (1.0 / patches), wo[...])
    rfull = lax.broadcasted_iota(jnp.int32, (fp, width), 0)
    following = jnp.where(rfull < tm - 1, pltpu.roll(pooled, fp - 1, 0), 0.0)
    action = dot(pooled, w_pair[0], precision=HIGH) + dot(following, w_pair[1], precision=HIGH)
    quantized = dot(onehot[:, :n_codes], codebook[...], precision=HIGH)
    diff = action - quantized
    d_action = (2.0 * BETA) * diff
    pack[0] = pooled
    pack[1] = following
    pack[2] = jnp.zeros((fp, width), F32)
    pack[2, :, 0:latent] = diff
    pack[2, :, LANES : 2 * LANES] = onehot
    d_own = dot(d_action, w_pair[0], 1, 1, precision=HIGH)
    d_next = dot(d_action, w_pair[1], 1, 1, precision=HIGH)
    carried = jnp.where((rfull > 0) & (rfull < tm), pltpu.roll(d_next, 1, 0), 0.0)
    d_pooled = d_own + carried
    d_rows[...] = d_pooled
    d_att[...] = dot_split(d_pooled, wo[...], 1).astype(BF16)
    for r in range(1, dp):
        go(remote(pack, pack_all.at[i], ("pack", r), (i + r) % dp, t))

    mrow = lax.broadcasted_iota(jnp.int32, (total, fp), 0)
    mcol = lax.broadcasted_iota(jnp.int32, (total, fp), 1)
    spread = jnp.where(mrow // mine == mcol, 1.0, 0.0).astype(BF16)

    def backward(b, carry):
        q, k, v = (qkv[:, lanes_at(b, n)] for n in range(3))
        d_out = dot(spread, d_att[:, lanes_at(b, 0)]).astype(BF16)
        dq = dk = dv = jnp.zeros((total, LANES), F32)
        for j in range(per):
            w = probs[b * per + j]
            d_w = dot(only(d_out, j), v, 1, 1).astype(BF16).astype(F32)
            wd = w * d_w
            d_s = ((wd - w * jnp.sum(wd, axis=-1, keepdims=True)) * scale_q).astype(BF16)
            dq = dq + dot(d_s, only(k, j))
            dk = dk + dot(d_s, only(q, j), 0, 0)
            dv = dv + dot(w.astype(BF16), only(d_out, j), 0, 0)
        dqkv[:, lanes_at(b, 0)] = dq.astype(BF16)
        dqkv[:, lanes_at(b, 1)] = dk.astype(BF16)
        dqkv[:, lanes_at(b, 2)] = dv.astype(BF16)
        return carry

    lax.fori_loop(0, width // LANES, backward, 0)

    pieces = dn_send.shape[0]
    wide = width // pieces
    for c in range(pieces):
        dn_send[c] = dot(dqkv[...], wq[c * wide : (c + 1) * wide, :], 1, 1).astype(BF16)
        for r in sorted(range(1, tm), key=lambda r: -min(r, tm - r)):
            other = (t + r) % tm
            go(remote(
                dn_send.at[c, pl.ds(pl.multiple_of(other * mine, mine), mine)],
                dn_recv.at[c, pl.ds(pl.multiple_of(t * mine, mine), mine)], ("dn", c, r), i, other,
            ))
        at = pl.ds(pl.multiple_of(t * mine, mine), mine)
        dn_recv[c, at, :] = dn_send[c, at, :]

    pack_all[i] = pack[...]
    for r in range(1, dp):
        remote(pack, pack_all.at[i], ("pack", r), i, t).wait_recv()
    every = dp * fp
    now_all = pack_all[:, 0].reshape(every, width)
    next_all = pack_all[:, 1].reshape(every, width)
    diff_all = pack_all[:, 2, :, :LANES].reshape(every, LANES)
    hot_all = pack_all[:, 2, :, LANES : 2 * LANES].reshape(every, LANES)
    da_all = (2.0 * BETA) * diff_all
    pair_out[0] = dot(da_all, now_all, 0, 0, precision=HIGH)[:latent]
    pair_out[1] = dot(da_all, next_all, 0, 0, precision=HIGH)[:latent]
    code_total = dot(hot_all, -2.0 * diff_all, 0, 0, precision=HIGH)
    count = dot(hot_all, jnp.ones((every, LANES), F32), 0, 0, precision=HIGH)
    step_out[...] = code_total[:n_codes, :latent] / count[:n_codes, :latent]

    for c in range(pieces):
        for r in range(1, tm):
            remote(
                dn_send.at[c, pl.ds(0, mine)],
                dn_recv.at[c, pl.ds(pl.multiple_of(t * mine, mine), mine)], ("dn", c, r), i, t,
            ).wait_recv()
    d_resid = d_rows[pl.ds(t, 1), :]

    def finish(b, carry):
        at = pl.ds(pl.multiple_of(b * block, block), block)
        xf = tokens[at, :].astype(F32)
        scale = lax.rsqrt(jnp.mean(xf * xf, axis=-1, keepdims=True) + EPS)
        dn = jnp.concatenate([dn_recv[c, at, :] for c in range(pieces)], axis=1).astype(F32)
        u = dn * gain[...].astype(F32)
        inner = jnp.mean(xf * u, axis=-1, keepdims=True)
        dx = u * scale - xf * (scale * scale * scale * inner)
        out[at, :] = (d_resid + dx).astype(BF16)
        return carry

    lax.fori_loop(0, total // block, finish, 0)
    for copy in started:
        copy.wait_send()
    assert len(tags) <= send.shape[0]


def local(dp, tm, tokens, gain, w_qkv, w_out, w_pair, codebook, codes):
    patches, width = tokens.shape[2:]
    rows = w_qkv.shape[0]
    latent, n_codes = w_pair.shape[2], codebook.shape[0]
    fp = -(-tm // 8) * 8
    heads = width // HEAD_DIM
    pieces = 4
    tags = (tm - 1) * (2 + pieces) + (dp - 1) + 8 * dp + 16
    vmem = pl.BlockSpec(memory_space=pltpu.VMEM)
    grad, pair, step = pl.pallas_call(
        functools.partial(kernel, (dp, tm, rows, patches, width, latent, n_codes)),
        out_shape=(
            jax.ShapeDtypeStruct((patches, width), BF16),
            jax.ShapeDtypeStruct((2, latent, width), F32),
            jax.ShapeDtypeStruct((n_codes, latent), F32),
        ),
        in_specs=[vmem] * 6 + [pl.BlockSpec(memory_space=pltpu.SMEM)],
        out_specs=(vmem, vmem, vmem),
        scratch_shapes=[
            pltpu.VMEM((dp * rows, 3 * width), BF16),
            pltpu.VMEM((dp * rows, width), BF16),
            pltpu.VMEM((patches, width), BF16),
            pltpu.VMEM((patches, width), BF16),
            pltpu.VMEM((patches, 3 * width), F32),
            pltpu.VMEM((patches, 3 * width), BF16),
            pltpu.VMEM((patches, patches), F32),
            pltpu.VMEM((heads, patches, patches), F32),
            pltpu.VMEM((patches, width), BF16),
            pltpu.VMEM((3, fp, width), F32),
            pltpu.VMEM((tm, 3, fp, width), F32),
            pltpu.VMEM((3, fp, width), F32),
            pltpu.VMEM((dp, 3, fp, width), F32),
            pltpu.VMEM((fp, width), F32),
            pltpu.VMEM((fp, width), BF16),
            pltpu.VMEM((patches, 3 * width), BF16),
            pltpu.VMEM((pieces, patches, width // pieces), BF16),
            pltpu.VMEM((pieces, patches, width // pieces), BF16),
            pltpu.SemaphoreType.DMA((tags,)),
            pltpu.SemaphoreType.DMA((tags,)),
            pltpu.SemaphoreType.DMA((3,)),
        ],
        compiler_params=pltpu.CompilerParams(
            collective_id=0, has_side_effects=True, vmem_limit_bytes=60 * 1024 * 1024
        ),
    )(
        tokens.reshape(patches, width), gain.reshape(1, width), w_qkv, w_out, w_pair, codebook,
        codes.reshape(1, 1),
    )
    return grad.reshape(tokens.shape), pair.swapaxes(1, 2), step


def solution(mesh):
    placed = (
        P("dp", "tm", None, None),
        P(),
        P("dp", None),
        P("dp", None),
        P(),
        P(),
        P("dp", "tm", None),
    )
    return jax.shard_map(
        functools.partial(local, mesh.shape["dp"], mesh.shape["tm"]),
        mesh=mesh,
        in_specs=placed,
        out_specs=(P("dp", "tm", None, None), P(), P()),
        check_vma=False,
    )
```

time: 301 us -> 84.7 us (0.28)
  waiting for transfers between devices: 156 us -> 0 us
  Pallas kernels: 0 us -> 76.4 us
  blocking collectives: 39.8 us -> 0 us
  matrix products: 32.2 us -> 0 us
  starting transfers between devices: 21.3 us -> 0 us
  other arithmetic: 16.1 us -> 0 us
  local copies, waits for them, and re-layouts: 20.4 us -> 6.74 us
  between operations: 14.8 us -> 1.31 us
    psum x1 -> x0, waiting for transfers between devices: 91.1 us -> none  [local(): lax.psum((pair_part, code_part, count_part), ('dp', 'tm'))]
    pallas_call x0 -> x1, Pallas kernels: none -> 76.4 us  [local(): pl.pallas_call(functools.partial(kernel, (dp, tm, rows, patches, width, l...]
    psum x1 -> x0, blocking collectives: 39.8 us -> none  [local(): lax.psum((pair_part, code_part, count_part), ('dp', 'tm'))]
    all_to_all x4 -> x0, waiting for transfers between devices: 38.7 us -> none  [the longest x1 13.7 us: local(): lax.all_to_all(normed, 'tm', split_axis=2, concat_axis=1, tiled=True)]
    dot_general x14 -> x0, matrix products: 26.8 us -> none  [the longest x2 11.7 us: project(): jnp.dot(normed.reshape(-1, shape[-1]), weight, preferred_element_type=jnp...]
    all_gather x2 -> x0, waiting for transfers between devices: 19.6 us -> none  [the longest x1 19.1 us: local(): lax.all_gather(w_qkv, 'dp', axis=0, tiled=True)]
    all_to_all x4 -> x0, starting transfers between devices: 18.2 us -> none  [the longest x1 6.35 us: local(): lax.all_to_all(normed, 'tm', split_axis=2, concat_axis=1, tiled=True)]
    reshape x3 -> x1, local copies, waits for them, and re-layouts: 8.54 us -> 0.6 us  [local(): gain.reshape(1, width)]
  transfers between devices with their start and end apart: 9 -> 0, of which waited for: 8 -> 0; matrix products, arithmetic and copies ran while one was open for 12% -> 0% of each run, Pallas kernels for 0% -> 0%
where the time goes in v1:
time: 84.7 us; the launch traced here: 84.5 us
  Pallas kernels  76.4 us (90%)
  local copies, waits for them, and re-layouts  6.74 us (8%)
  between operations  1.31 us (2%)
    pallas_call x1, Pallas kernels, local(): pl.pallas_call(functools.partial(kernel, (dp, tm, rows, patches, width, l...  76.4 us
    unnamed x10, local copies, waits for them, and re-layouts  6.14 us

profile of v1, /device:TPU:0, one launch (start us, length us, event | category | flops | bytes accessed | tf_op | source)
XLA Modules:
  0.0 84.5 jit_solution(8719376917252429722)
XLA Ops:
  1.3 0.0 copy-start.2
  1.3 0.7 copy-done.2
  2.0 0.6 reshape.19.gain
  2.6 2.3 %copy.10.w_pair = f32[2,1024,32]{2,1,0:T(8,128)} copy(f32[2,1024,32]{1,2,0:T(8,128)} %param.11) | data formatting | bytes 524288 | tf_op args[4]
  4.8 76.4 %shard_map.94 = (bf16[256,1024]{1,0:T(8,128)(2,1)}, f32[2,32,1024]{2,1,0:T(8,128)}, f32[8,32]{1,0:T(8,128)}) custom-call(bf16[256,1024]{1,0:T(8,128)(2,1)} %bitcast.6, bf16[1,1024]{1,0:T(2,128)(2,1)} %reshape.19.gain, bf16[128,3072]{1,0:T(8,128)(2,1)} %wq_own.1, bf16[128,1024]{1,0:T(8,128)(2,1)} %wo_own.1, f32[2,1024,32]{2,1,0:T(8,128)} %copy.10.w_pair, ...), custom_call_target="tpu_custom_call" | custom-call | tf_op jit(solution)/shard_map/pallas_call | solution.py:402
  81.3 0.0 copy-start
  81.3 1.9 %copy.15 = bf16[1,1,256,1024]{3,2,1,0:T(8,128)(2,1)} copy(bf16[1,1,256,1024]{3,2,1,0:T(8,128)(2,1)} %bitcast.5) | data formatting | bytes 1048576
  83.2 0.0 copy-done
  83.2 0.0 copy-start.1
  83.2 0.7 copy.16
  83.9 0.0 copy-done.1
  83.9 0.6 copy.17
Async XLA Ops:
  1.3 0.7 copy-start.2
  81.3 1.9 %copy-start = (f32[2,32,1024]{2,1,0:T(8,128)S(1)}, f32[2,32,1024]{2,1,0:T(8,128)}, u32[]{:S(2)}) copy-start(f32[2,32,1024]{2,1,0:T(8,128)} %get-tuple-element.7) | copy-start | bytes 786436
  83.2 0.7 copy-start.1

commit v2 on v1

--- a/solution.py
+++ b/solution.py
@@ -54,9 +54,11 @@
     wq, wo, x, normed, acc, qkv, bias, probs, attended, sums, sums_all, pack, pack_all,
     d_rows, d_att, dqkv, dn_send, dn_recv, send, recv, local_sem,
 ):
-    dp, tm, rows, patches, width, latent, n_codes = cfg
+    dp, tm, rows, patches, width, latent, n_codes, groups = cfg
     mine = patches // tm
     total = tm * mine
+    sub = mine // groups
+    part_rows = tm * sub
     fp = sums.shape[1]
     chips = dp // 2
     half_ring = chips // 2
@@ -98,11 +100,26 @@
     half = rows // 2
     dirs = (1, -1)
 
+    quarter = half // 2
+    sharing = half_ring == 2 and quarter % 16 == 0 and tm % 2 == 0
+    odd = t % 2
+    twin = t + 1 - 2 * odd
+
     def piece(m, origin, h):
         return mats[m].at[pl.ds(pl.multiple_of(origin * rows + h * half, half), half)]
 
     def own_piece(m, h):
         return owns[m].at[pl.ds(h * half, half)]
+
+    def split(m, d, s, h):
+        return sharing and m == 0 and s == 0 and h != main_half(d)
+
+    def quarter_of(m, origin, h, which):
+        at = origin * rows + h * half + which * quarter
+        return mats[m].at[pl.ds(pl.multiple_of(at, quarter), quarter)]
+
+    def own_quarter(m, h, which):
+        return owns[m].at[pl.ds(pl.multiple_of(h * half + which * quarter, quarter), quarter)]
 
     def main_half(d):
         return 0 if dirs[d] == 1 else 1
@@ -113,6 +130,11 @@
 
     def ring_copy(m, d, s, h):
         origin = device_at(place - dirs[d] * s, core)
+        if split(m, d, s, h):
+            return remote(
+                own_quarter(m, h, odd), quarter_of(m, origin, h, odd), ("ring", m, d, s, h),
+                device_at(place + dirs[d], core), t,
+            )
         src = own_piece(m, h) if s == 0 else piece(m, origin, h)
         return remote(src, piece(m, origin, h), ("ring", m, d, s, h), device_at(place + dirs[d], core), t)
 
@@ -120,6 +142,17 @@
         origin = device_at(place - dirs[d] * s, core)
         src = own_piece(m, h) if s == 0 else piece(m, origin, h)
         return remote(src, piece(m, origin, h), ("sib", m, d, s, h), device_at(place, 1 - core), t)
+
+    def twin_copy(d):
+        h = 1 - main_half(d)
+        at = quarter_of(0, device_at(place - dirs[d], core), h, odd)
+        return remote(at, at, ("twin", d), i, twin)
+
+    def quarter_sib(d, n):
+        h = 1 - main_half(d)
+        which = odd if n == 0 else 1 - odd
+        at = quarter_of(0, device_at(place - dirs[d], core), h, which)
+        return remote(at, at, ("quarter", d, n), device_at(place, 1 - core), t)
 
     def start_own(m):
         for n in range(2):
@@ -131,43 +164,39 @@
 
     def take(m, d, s, h):
         ring_copy(m, d, s, h).wait_recv()
+        if split(m, d, s, h):
+            go(twin_copy(d))
+            go(quarter_sib(d, 0))
+            return
         if s + 1 < half_ring and h in halves(d, s + 1):
             go(ring_copy(m, d, s + 1, h))
         go(sib_copy(m, d, s + 1, h))
 
     for r in sorted(range(1, tm), key=lambda r: -min(r, tm - r)):
         other = (t + r) % tm
-        go(remote(
-            tokens.at[pl.ds(pl.multiple_of(other * mine, mine), mine)],
-            x.at[pl.ds(pl.multiple_of(t * mine, mine), mine)], ("tok", r), i, other,
-        ))
+        for g in range(groups):
+            go(remote(
+                tokens.at[pl.ds(pl.multiple_of(other * mine + g * sub, sub), sub)],
+                x.at[pl.ds(pl.multiple_of(g * part_rows + t * sub, sub), sub)], ("tok", r, g), i, other,
+            ))
     start_own(0)
     here = [
         pltpu.make_async_copy(wq_own, wq.at[pl.ds(pl.multiple_of(i * rows, rows), rows)], local_sem.at[0]),
         pltpu.make_async_copy(wo_own, wo.at[pl.ds(pl.multiple_of(i * rows, rows), rows)], local_sem.at[1]),
+    ] + [
         pltpu.make_async_copy(
-            tokens.at[pl.ds(pl.multiple_of(t * mine, mine), mine)],
-            x.at[pl.ds(pl.multiple_of(t * mine, mine), mine)], local_sem.at[2],
-        ),
+            tokens.at[pl.ds(pl.multiple_of(t * mine + g * sub, sub), sub)],
+            x.at[pl.ds(pl.multiple_of(g * part_rows + t * sub, sub), sub)], local_sem.at[2 + g],
+        )
+        for g in range(groups)
     ]
     for copy in here:
         copy.start()
 
-    row = lax.broadcasted_iota(jnp.int32, (total, total), 0)
-    col = lax.broadcasted_iota(jnp.int32, (total, total), 1)
-    seen = (row % mine == col % mine) & (row // mine >= col // mine)
+    row = lax.broadcasted_iota(jnp.int32, (part_rows, part_rows), 0)
+    col = lax.broadcasted_iota(jnp.int32, (part_rows, part_rows), 1)
+    seen = (row % sub == col % sub) & (row // sub >= col // sub)
     bias[...] = jnp.where(seen, 0.0, -1e30).astype(F32)
-
-    def first_main(m):
-        for s in range(half_ring):
-            for d in range(2):
-                take(m, d, s, main_half(d))
-
-    def rest_of(m):
-        for s in range(half_ring):
-            for d in range(2):
-                for h in halves(d, s)[1:]:
-                    take(m, d, s, h)
 
     if half_ring > 1:
         for d in range(2):
@@ -177,9 +206,11 @@
     for copy in here:
         copy.wait()
     for r in range(1, tm):
-        remote(
-            tokens.at[pl.ds(0, mine)], x.at[pl.ds(pl.multiple_of(t * mine, mine), mine)], ("tok", r), i, t
-        ).wait_recv()
+        for g in range(groups):
+            remote(
+                tokens.at[pl.ds(0, sub)], x.at[pl.ds(pl.multiple_of(g * part_rows + t * sub, sub), sub)],
+                ("tok", r, g), i, t,
+            ).wait_recv()
 
     block = 32
 
@@ -191,6 +222,14 @@
         return carry
 
     lax.fori_loop(0, total // block, norm_step, 0)
+
+    frow = lax.broadcasted_iota(jnp.int32, (fp, total), 0)
+    fcol = lax.broadcasted_iota(jnp.int32, (fp, total), 1)
+    member = jnp.where((fcol % part_rows) // sub == frow, 1.0, 0.0).astype(BF16)
+    sums[1] = dot(member, x[...])
+    r8 = lax.broadcasted_iota(jnp.int32, (fp, width), 0)
+    l8 = lax.broadcasted_iota(jnp.int32, (fp, width), 1)
+    sums[2] = jnp.where((r8 == t) & (l8 == codes[0, 0]), 1.0, 0.0).astype(F32)
 
     pair = 2 * rows
     columns = 512
@@ -219,16 +258,36 @@
         wait_sib(0, 0, 0, h)
     if by_chip:
         project(place, True, chips == 1)
-    for s in range(half_ring):
-        for d in range(2):
-            for n, h in enumerate(halves(d, s)):
-                if not (half_ring > 1 and s == 0 and n == 0):
-                    take(0, d, s, h)
-        for d in range(2):
-            for h in halves(d, s):
-                wait_sib(0, d, s + 1, h)
-            if by_chip and s < half_ring - 1:
-                project(place - dirs[d] * (s + 1), False, False)
+    if sharing:
+        for d in range(2):
+            take(0, d, 0, 1 - main_half(d))
+        for d in range(2):
+            twin_copy(d).wait_recv()
+            go(quarter_sib(d, 1))
+        for d in range(2):
+            wait_sib(0, d, 1, main_half(d))
+            for n in range(2):
+                quarter_sib(d, n).wait_recv()
+            if by_chip:
+                project(place - dirs[d], False, False)
+            if d == 0:
+                for e in range(2):
+                    take(0, e, 1, main_half(e))
+        for d in range(2):
+            wait_sib(0, d, 2, main_half(d))
+    else:
+        for s in range(half_ring):
+            for d in range(2):
+                for n, h in enumerate(halves(d, s)):
+                    if not (half_ring > 1 and s == 0 and n == 0):
+                        take(0, d, s, h)
+            for d in range(2):
+                for h in halves(d, s):
+                    wait_sib(0, d, s + 1, h)
+                if by_chip and s < half_ring - 1:
+                    project(place - dirs[d] * (s + 1), False, False)
+    for r in range(1, tm):
+        go(remote(sums.at[pl.ds(1, 2)], sums_all.at[t, pl.ds(1, 2)], ("early", r), i, (t + r) % tm))
     if by_chip:
         project(place + half_ring, False, True)
     else:
@@ -239,46 +298,52 @@
 
         lax.fori_loop(0, 3 * width // columns, whole_body, 0)
 
+    if half_ring > 1:
+        for d in range(2):
+            take(1, d, 0, main_half(d))
+
     per = LANES // HEAD_DIM
-    lane = lax.broadcasted_iota(jnp.int32, (total, LANES), 1)
+    lane = lax.broadcasted_iota(jnp.int32, (part_rows, LANES), 1)
     scale_q = HEAD_DIM ** (-0.5)
 
     def only(value, j):
         return jnp.where(lane // HEAD_DIM == j, value, jnp.zeros_like(value))
 
     def lanes_at(b, part):
-        return pl.ds(pl.multiple_of(part * width + b * LANES, LANES), LANES)
-
-    def forward(b, carry):
-        q, k, v = (qkv[:, lanes_at(b, n)] for n in range(3))
-        mixed = None
-        for j in range(per):
-            scores = dot(only(q, j), k, 1, 1) * scale_q + bias[...]
-            e = jnp.exp(scores - jnp.max(scores, axis=-1, keepdims=True))
-            w = e / jnp.sum(e, axis=-1, keepdims=True)
-            probs[b * per + j] = w
-            term = dot(w.astype(BF16), only(v, j))
-            mixed = term if mixed is None else mixed + term
-        attended[:, lanes_at(b, 0)] = mixed.astype(BF16)
-        return carry
-
-    lax.fori_loop(0, width // LANES, forward, 0)
-
-    frow = lax.broadcasted_iota(jnp.int32, (fp, total), 0)
-    fcol = lax.broadcasted_iota(jnp.int32, (fp, total), 1)
-    member = jnp.where(fcol // mine == frow, 1.0, 0.0).astype(BF16)
+        return pl.ds(part * width + b * LANES, LANES)
+
+    heads = width // HEAD_DIM
+
+    def group(g):
+        return pl.ds(g * part_rows, part_rows)
+
+    def forward(b):
+        chains = [(g, j) for g in range(groups) for j in range(per)]
+        q, k, v = ([qkv[group(g), lanes_at(b, n)] for g in range(groups)] for n in range(3))
+        scores = [dot(only(q[g], j), k[g], 1, 1) * scale_q + bias[...] for g, j in chains]
+        tops = [jnp.max(value, axis=-1, keepdims=True) for value in scores]
+        raised = [jnp.exp(value - top) for value, top in zip(scores, tops)]
+        totals = [jnp.sum(value, axis=-1, keepdims=True) for value in raised]
+        ws = [value / whole for value, whole in zip(raised, totals)]
+        for (g, j), w in zip(chains, ws):
+            probs[g * heads + b * per + j] = w
+        terms = [dot(w.astype(BF16), only(v[g], j)) for (g, j), w in zip(chains, ws)]
+        for g in range(groups):
+            attended[group(g), lanes_at(b, 0)] = sum(terms[g * per + 1 : g * per + per], terms[g * per]).astype(BF16)
+
+    blocks = width // LANES
+    for b in range(blocks):
+        forward(b)
+
     sums[0] = dot(member, attended[...])
-    sums[1] = dot(member, x[...])
-    r8 = lax.broadcasted_iota(jnp.int32, (fp, width), 0)
-    l8 = lax.broadcasted_iota(jnp.int32, (fp, width), 1)
-    sums[2] = jnp.where((r8 == t) & (l8 == codes[0, 0]), 1.0, 0.0).astype(F32)
     for r in range(1, tm):
-        go(remote(sums, sums_all.at[t], ("sum", r), i, (t + r) % tm))
+        go(remote(sums.at[0], sums_all.at[t, 0], ("sum", r), i, (t + r) % tm))
 
     for s in range(half_ring):
         for d in range(2):
-            for h in halves(d, s):
-                take(1, d, s, h)
+            for n, h in enumerate(halves(d, s)):
+                if not (half_ring > 1 and s == 0 and n == 0):
+                    take(1, d, s, h)
     sums_all[t] = sums[...]
     for h in range(2):
         wait_sib(1, 0, 0, h)
@@ -287,7 +352,8 @@
             for h in halves(d, s):
                 wait_sib(1, d, s + 1, h)
     for r in range(1, tm):
-        remote(sums, sums_all.at[t], ("sum", r), i, t).wait_recv()
+        remote(sums.at[0], sums_all.at[t, 0], ("sum", r), i, t).wait_recv()
+        remote(sums.at[pl.ds(1, 2)], sums_all.at[t, pl.ds(1, 2)], ("early", r), i, t).wait_recv()
 
     tot = sums_all[0]
     for r in range(1, tm):
@@ -296,7 +362,7 @@
     pooled = tot[1] * (1.0 / patches) + dot_split(tot[0] * (1.0 / patches), wo[...])
     rfull = lax.broadcasted_iota(jnp.int32, (fp, width), 0)
     following = jnp.where(rfull < tm - 1, pltpu.roll(pooled, fp - 1, 0), 0.0)
-    action = dot(pooled, w_pair[0], precision=HIGH) + dot(following, w_pair[1], precision=HIGH)
+    action = dot(pooled, w_pair[0], 1, 1, HIGH) + dot(following, w_pair[1], 1, 1, HIGH)
     quantized = dot(onehot[:, :n_codes], codebook[...], precision=HIGH)
     diff = action - quantized
     d_action = (2.0 * BETA) * diff
@@ -305,8 +371,8 @@
     pack[2] = jnp.zeros((fp, width), F32)
     pack[2, :, 0:latent] = diff
     pack[2, :, LANES : 2 * LANES] = onehot
-    d_own = dot(d_action, w_pair[0], 1, 1, precision=HIGH)
-    d_next = dot(d_action, w_pair[1], 1, 1, precision=HIGH)
+    d_own = dot(d_action, w_pair[0], precision=HIGH)
+    d_next = dot(d_action, w_pair[1], precision=HIGH)
     carried = jnp.where((rfull > 0) & (rfull < tm), pltpu.roll(d_next, 1, 0), 0.0)
     d_pooled = d_own + carried
     d_rows[...] = d_pooled
@@ -314,41 +380,45 @@
     for r in range(1, dp):
         go(remote(pack, pack_all.at[i], ("pack", r), (i + r) % dp, t))
 
-    mrow = lax.broadcasted_iota(jnp.int32, (total, fp), 0)
-    mcol = lax.broadcasted_iota(jnp.int32, (total, fp), 1)
-    spread = jnp.where(mrow // mine == mcol, 1.0, 0.0).astype(BF16)
-
-    def backward(b, carry):
-        q, k, v = (qkv[:, lanes_at(b, n)] for n in range(3))
-        d_out = dot(spread, d_att[:, lanes_at(b, 0)]).astype(BF16)
-        dq = dk = dv = jnp.zeros((total, LANES), F32)
-        for j in range(per):
-            w = probs[b * per + j]
-            d_w = dot(only(d_out, j), v, 1, 1).astype(BF16).astype(F32)
-            wd = w * d_w
-            d_s = ((wd - w * jnp.sum(wd, axis=-1, keepdims=True)) * scale_q).astype(BF16)
-            dq = dq + dot(d_s, only(k, j))
-            dk = dk + dot(d_s, only(q, j), 0, 0)
-            dv = dv + dot(w.astype(BF16), only(d_out, j), 0, 0)
-        dqkv[:, lanes_at(b, 0)] = dq.astype(BF16)
-        dqkv[:, lanes_at(b, 1)] = dk.astype(BF16)
-        dqkv[:, lanes_at(b, 2)] = dv.astype(BF16)
-        return carry
-
-    lax.fori_loop(0, width // LANES, backward, 0)
+    mrow = lax.broadcasted_iota(jnp.int32, (part_rows, fp), 0)
+    mcol = lax.broadcasted_iota(jnp.int32, (part_rows, fp), 1)
+    spread = jnp.where(mrow // sub == mcol, 1.0, 0.0).astype(BF16)
+
+    def backward(g, near):
+        chains = [(b, j) for b in near for j in range(per)]
+        q, k, v = ({b: qkv[group(g), lanes_at(b, n)] for b in near} for n in range(3))
+        d_out = {b: dot(spread, d_att[:, lanes_at(b, 0)]).astype(BF16) for b in near}
+        ws = [probs[g * heads + b * per + j] for b, j in chains]
+        d_ws = [dot(only(d_out[b], j), v[b], 1, 1).astype(BF16).astype(F32) for b, j in chains]
+        wds = [w * d_w for w, d_w in zip(ws, d_ws)]
+        means = [jnp.sum(wd, axis=-1, keepdims=True) for wd in wds]
+        d_ss = [((wd - w * m) * scale_q).astype(BF16) for wd, w, m in zip(wds, ws, means)]
+        dqs = [dot(d_s, only(k[b], j)) for (b, j), d_s in zip(chains, d_ss)]
+        dks = [dot(d_s, only(q[b], j), 0, 0) for (b, j), d_s in zip(chains, d_ss)]
+        dvs = [dot(w.astype(BF16), only(d_out[b], j), 0, 0) for (b, j), w in zip(chains, ws)]
+        for n, b in enumerate(near):
+            for part, terms in enumerate((dqs, dks, dvs)):
+                mine_terms = terms[n * per : (n + 1) * per]
+                dqkv[group(g), lanes_at(b, part)] = sum(mine_terms[1:], mine_terms[0]).astype(BF16)
+
+    def dn_copy(c, g, r, other):
+        return remote(
+            dn_send.at[c, pl.ds(pl.multiple_of(g * part_rows + other * sub, sub), sub)],
+            dn_recv.at[c, pl.ds(pl.multiple_of(t * mine + g * sub, sub), sub)], ("dn", c, g, r), i, other,
+        )
 
     pieces = dn_send.shape[0]
     wide = width // pieces
-    for c in range(pieces):
-        dn_send[c] = dot(dqkv[...], wq[c * wide : (c + 1) * wide, :], 1, 1).astype(BF16)
-        for r in sorted(range(1, tm), key=lambda r: -min(r, tm - r)):
-            other = (t + r) % tm
-            go(remote(
-                dn_send.at[c, pl.ds(pl.multiple_of(other * mine, mine), mine)],
-                dn_recv.at[c, pl.ds(pl.multiple_of(t * mine, mine), mine)], ("dn", c, r), i, other,
-            ))
-        at = pl.ds(pl.multiple_of(t * mine, mine), mine)
-        dn_recv[c, at, :] = dn_send[c, at, :]
+    for g in range(groups):
+        for b in range(0, blocks, 2):
+            backward(g, tuple(range(b, min(b + 2, blocks))))
+        for c in range(pieces):
+            dn_send[c, group(g), :] = dot(dqkv[group(g), :], wq[c * wide : (c + 1) * wide, :], 1, 1).astype(BF16)
+            for r in sorted(range(1, tm), key=lambda r: -min(r, tm - r)):
+                go(dn_copy(c, g, r, (t + r) % tm))
+            dn_recv[c, pl.ds(pl.multiple_of(t * mine + g * sub, sub), sub), :] = dn_send[
+                c, pl.ds(pl.multiple_of(g * part_rows + t * sub, sub), sub), :
+            ]
 
     pack_all[i] = pack[...]
     for r in range(1, dp):
@@ -365,12 +435,10 @@
     count = dot(hot_all, jnp.ones((every, LANES), F32), 0, 0, precision=HIGH)
     step_out[...] = code_total[:n_codes, :latent] / count[:n_codes, :latent]
 
-    for c in range(pieces):
-        for r in range(1, tm):
-            remote(
-                dn_send.at[c, pl.ds(0, mine)],
-                dn_recv.at[c, pl.ds(pl.multiple_of(t * mine, mine), mine)], ("dn", c, r), i, t,
-            ).wait_recv()
+    for g in range(groups):
+        for c in range(pieces):
+            for r in range(1, tm):
+                dn_copy(c, g, r, t).wait_recv()
     d_resid = d_rows[pl.ds(t, 1), :]
 
     def finish(b, carry):
@@ -396,11 +464,13 @@
     latent, n_codes = w_pair.shape[2], codebook.shape[0]
     fp = -(-tm // 8) * 8
     heads = width // HEAD_DIM
-    pieces = 4
-    tags = (tm - 1) * (2 + pieces) + (dp - 1) + 8 * dp + 16
+    pieces = 2
+    groups = 2 if patches // tm % 32 == 0 else 1
+    part_rows = patches // groups
+    tags = (tm - 1) * (2 + groups + groups * pieces) + (dp - 1) + 8 * dp + 16
     vmem = pl.BlockSpec(memory_space=pltpu.VMEM)
     grad, pair, step = pl.pallas_call(
-        functools.partial(kernel, (dp, tm, rows, patches, width, latent, n_codes)),
+        functools.partial(kernel, (dp, tm, rows, patches, width, latent, n_codes, groups)),
         out_shape=(
             jax.ShapeDtypeStruct((patches, width), BF16),
             jax.ShapeDtypeStruct((2, latent, width), F32),
@@ -415,8 +485,8 @@
             pltpu.VMEM((patches, width), BF16),
             pltpu.VMEM((patches, 3 * width), F32),
             pltpu.VMEM((patches, 3 * width), BF16),
-            pltpu.VMEM((patches, patches), F32),
-            pltpu.VMEM((heads, patches, patches), F32),
+            pltpu.VMEM((part_rows, part_rows), F32),
+            pltpu.VMEM((groups * heads, part_rows, part_rows), F32),
             pltpu.VMEM((patches, width), BF16),
             pltpu.VMEM((3, fp, width), F32),
             pltpu.VMEM((tm, 3, fp, width), F32),
@@ -429,13 +499,13 @@
             pltpu.VMEM((pieces, patches, width // pieces), BF16),
             pltpu.SemaphoreType.DMA((tags,)),
             pltpu.SemaphoreType.DMA((tags,)),
-            pltpu.SemaphoreType.DMA((3,)),
+            pltpu.SemaphoreType.DMA((2 + groups,)),
         ],
         compiler_params=pltpu.CompilerParams(
             collective_id=0, has_side_effects=True, vmem_limit_bytes=60 * 1024 * 1024
         ),
     )(
-        tokens.reshape(patches, width), gain.reshape(1, width), w_qkv, w_out, w_pair, codebook,
+        tokens.reshape(patches, width), gain.reshape(1, width), w_qkv, w_out, w_pair.swapaxes(1, 2), codebook,
         codes.reshape(1, 1),
     )
     return grad.reshape(tokens.shape), pair.swapaxes(1, 2), step

time: 84.7 us -> 72.6 us (0.86)
  Pallas kernels: 76.4 us -> 66.6 us
  local copies, waits for them, and re-layouts: 6.74 us -> 4.48 us
    pallas_call x1, Pallas kernels: 76.4 us -> 66.6 us  [local(): pl.pallas_call(functools.partial(kernel, (dp, tm, rows, patches, width, l...]
    unnamed x10 -> x9, local copies, waits for them, and re-layouts: 6.14 us -> 3.89 us
where the time goes in v2:
time: 72.6 us; the launch traced here: 72.4 us
  Pallas kernels  66.6 us (92%)
  local copies, waits for them, and re-layouts  4.48 us (6%)
  between operations  1.3 us (2%)
    pallas_call x1, Pallas kernels, local(): pl.pallas_call(functools.partial(kernel, (dp, tm, rows, patches, width, l...  66.6 us
    unnamed x9, local copies, waits for them, and re-layouts  3.89 us

profile of v2, /device:TPU:0, one launch (start us, length us, event | category | flops | bytes accessed | tf_op | source)
XLA Modules:
  0.0 72.4 jit_solution(7192662214745751865)
XLA Ops:
  1.3 0.0 copy-start.2
  1.3 0.7 copy-done.2
  2.0 0.6 reshape.19.gain
  2.6 66.6 %shard_map.94 = (bf16[256,1024]{1,0:T(8,128)(2,1)}, f32[2,32,1024]{2,1,0:T(8,128)}, f32[8,32]{1,0:T(8,128)}) custom-call(bf16[256,1024]{1,0:T(8,128)(2,1)} %bitcast.7, bf16[1,1024]{1,0:T(2,128)(2,1)} %reshape.19.gain, bf16[128,3072]{1,0:T(8,128)(2,1)} %wq_own.1, bf16[128,1024]{1,0:T(8,128)(2,1)} %wo_own.1, f32[2,32,1024]{2,1,0:T(8,128)} %bitcast.9, ...), custom_call_target="tpu_custom_call" | custom-call | tf_op jit(solution)/shard_map/pallas_call | solution.py:472
  69.1 0.0 copy-start
  69.2 1.9 %copy.14 = bf16[1,1,256,1024]{3,2,1,0:T(8,128)(2,1)} copy(bf16[1,1,256,1024]{3,2,1,0:T(8,128)(2,1)} %bitcast.6) | data formatting | bytes 1048576
  71.1 0.0 copy-done
  71.1 0.0 copy-start.1
  71.1 0.7 copy.15
  71.8 0.0 copy-done.1
  71.8 0.6 copy.16
Async XLA Ops:
  1.3 0.7 copy-start.2
  69.1 1.9 %copy-start = (f32[2,32,1024]{2,1,0:T(8,128)S(1)}, f32[2,32,1024]{2,1,0:T(8,128)}, u32[]{:S(2)}) copy-start(f32[2,32,1024]{2,1,0:T(8,128)} %get-tuple-element.7) | copy-start | bytes 786436
  71.1 0.7 copy-start.1
